TPU v7x, 32 devices: a whole 2x2x4 slice. The times are simulated.
32 devices in a mesh: dp: 8 (over y, x, core), tensor: 4 (over z).
Axes of the slice: x: 2, y: 2, z: 4, core: 2. Of those that a mesh axis runs over, the one named last changes fastest.
Arguments:
- layer_input: bfloat16 [16384, 4096], P('dp', 'tensor'), may hold values from -54 to 54
- queries: bfloat16 [16384, 2048], P('dp', 'tensor'), may hold values from -6 to 6
- keys_values: bfloat16 [16384, 2, 1024], P('dp', None, 'tensor'), may hold values from -6 to 6
- out_grads: bfloat16 [16384, 2048], P('dp', 'tensor'), may hold values from -6 to 6
- log_sums: bfloat16 [16384, 16], P('dp', 'tensor'), may hold values from 2.5 to 5.5
- deltas: bfloat16 [16384, 16], P('dp', 'tensor'), may hold values from -1.5 to 1.5
- tile_fill: int32 [8, 16], replicated, may hold values from 1 to 128, as said below
- tile_cont: int32 [8, 16], replicated, may hold values from 0 to 1, as said below
- moment_first: float32 [4096, 2, 1024], P(('tensor', 'dp')), may hold values from -2 to 2
- moment_second: float32 [2, 8], replicated, may hold values from 0.05 to 0.5
Outputs:
- update: float32 [4096, 2, 1024], P(('tensor', 'dp'))
- new_first: float32 [4096, 2, 1024], P(('tensor', 'dp'))
- new_second: float32 [2, 8], replicated
Inputs may be any that keep to these rules, and one draw needn't show every extreme that they name: `tile_fill`: a tile followed by a tile with tile_cont 1 has all 128 positions live. Documents span one or two tiles: tile_cont is 0 for the first tile of each group and never 1 for two tiles in a row.
All inputs are finite; a program needn't handle non-finite values.
Results may differ from a plain program's by a relative error of at most 0.0055.
Values may be sent and summed in bfloat16 or wider, within the bound.
A program may use at most 64 MiB of HBM per device.

v0:
```python
import math
import jax
import jax.numpy as jnp
from jax import lax
from jax.sharding import PartitionSpec as P

D = 4096
HD = 128
ADAM_ONE = 0.9
ADAM_TWO = 0.95
ADAM_EPS = 1e-08


def band_grads(q_tiles, k_tiles, v_tiles, do_tiles, lse_tiles, delta_tiles, fill_tiles, cont_tiles):
    tile_total, block_len, groups, head_width = q_tiles.shape
    scale_qk = head_width ** (-0.5)
    zero_tile = jnp.zeros_like(k_tiles[:1])
    k_window = jnp.concatenate([jnp.concatenate([zero_tile, k_tiles[:-1]], 0), k_tiles], 1)
    v_window = jnp.concatenate([jnp.concatenate([zero_tile, v_tiles[:-1]], 0), v_tiles], 1)
    places = jnp.arange(block_len)
    live_rows = places[None, :] < fill_tiles[:, None]
    causal = places[:, None] >= places[None, :]
    own_part = live_rows[:, :, None] & causal[None]
    prev_part = (
        live_rows[:, :, None] & (cont_tiles[:, None, None] == 1) & (places[None, None, :] >= 0)
    )
    allowed = jnp.concatenate([prev_part, own_part], 2)[:, None]
    scores = (
        jnp.einsum("sqgd,skd->sgqk", q_tiles, k_window, preferred_element_type=jnp.float32)
        * scale_qk
    )
    lse_rows = jnp.swapaxes(lse_tiles.astype(jnp.float32), 1, 2)[..., None]
    delta_rows = jnp.swapaxes(delta_tiles.astype(jnp.float32), 1, 2)[..., None]
    prob_vals = jnp.where(allowed, jnp.exp(scores - lse_rows), 0.0)
    dprobs = jnp.einsum("sqgd,skd->sgqk", do_tiles, v_window, preferred_element_type=jnp.float32)
    dscores = prob_vals * (dprobs - delta_rows)
    value_grad = jnp.einsum(
        "sgqk,sqgd->skd",
        prob_vals.astype(jnp.bfloat16),
        do_tiles,
        preferred_element_type=jnp.float32,
    )
    key_grad = (
        jnp.einsum(
            "sgqk,sqgd->skd",
            dscores.astype(jnp.bfloat16),
            q_tiles,
            preferred_element_type=jnp.float32,
        )
        * scale_qk
    )
    key_out = key_grad[:, block_len:] + jnp.concatenate(
        [key_grad[1:, :block_len], jnp.zeros_like(key_grad[:1, :block_len])], 0
    )
    value_out = value_grad[:, block_len:] + jnp.concatenate(
        [value_grad[1:, :block_len], jnp.zeros_like(value_grad[:1, :block_len])], 0
    )
    return (key_out, value_out)


def attend_heads(q_tiles, kv_tiles, do_tiles, stat_tiles, fill_tiles, cont_tiles):
    tile_total, block_len = (q_tiles.shape[0], q_tiles.shape[1])
    kv_cols = kv_tiles.shape[3]
    kv_local = kv_cols // HD
    group_size = q_tiles.shape[2] // kv_cols
    q_heads = q_tiles.reshape(tile_total, block_len, kv_local, group_size, HD)
    do_heads = do_tiles.reshape(tile_total, block_len, kv_local, group_size, HD)
    stat_heads = stat_tiles.reshape(tile_total, block_len, 2, kv_local, group_size)
    results = []
    for head_index in range(kv_local):
        low_col = head_index * HD
        key_out, value_out = band_grads(
            q_heads[:, :, head_index],
            kv_tiles[:, :, 0, low_col : low_col + HD],
            kv_tiles[:, :, 1, low_col : low_col + HD],
            do_heads[:, :, head_index],
            stat_heads[:, :, 0, head_index],
            stat_heads[:, :, 1, head_index],
            fill_tiles,
            cont_tiles,
        )
        results.append(jnp.stack([key_out, value_out], 2))
    return jnp.concatenate(results, 3).astype(jnp.bfloat16)


def per_device(
    layer_input,
    queries,
    keys_values,
    out_grads,
    log_sums,
    deltas,
    tile_fill,
    tile_cont,
    moment_first,
    moment_second,
):
    group_count = lax.axis_size("dp")
    tile_count = tile_fill.shape[1]
    token_count = queries.shape[0]
    block_len = token_count // tile_count
    my_group = lax.axis_index("dp")
    q_tiles = queries.reshape(tile_count, block_len, -1)
    kv_tiles = keys_values.reshape(tile_count, block_len, 2, -1)
    do_tiles = out_grads.reshape(tile_count, block_len, -1)
    stat_tiles = jnp.stack([log_sums, deltas], 1).reshape(tile_count, block_len, 2, -1)
    fill_mine = lax.dynamic_index_in_dim(tile_fill, my_group, 0, keepdims=False)
    cont_mine = lax.dynamic_index_in_dim(tile_cont, my_group, 0, keepdims=False)
    kv_grads = attend_heads(q_tiles, kv_tiles, do_tiles, stat_tiles, fill_mine, cont_mine)
    kv_grads = kv_grads.reshape(token_count, 2, -1)
    terms = jnp.einsum(
        "tr,tkc->rkc",
        layer_input,
        lax.all_gather(kv_grads, "tensor", axis=2, tiled=True),
        preferred_element_type=jnp.float32,
    )
    summed = lax.psum_scatter(terms, "dp", scatter_dimension=0, tiled=True)
    proj_grads = summed / math.sqrt(token_count * group_count)
    new_first = ADAM_ONE * moment_first + (1 - ADAM_ONE) * proj_grads
    heads_kv = moment_second.shape[1]
    partial_squares = jnp.sum(
        jnp.square(proj_grads).reshape(proj_grads.shape[0], 2, heads_kv, -1), axis=(0, 3)
    )
    squares = lax.psum(partial_squares, ("dp", "tensor"))
    new_second = ADAM_TWO * moment_second + (1 - ADAM_TWO) * squares / (D * HD)
    step_size = jnp.sqrt(new_second / (1 - ADAM_TWO**2)) + ADAM_EPS
    scaled = (new_first / (1 - ADAM_ONE**2)).reshape(proj_grads.shape[0], 2, heads_kv, -1)
    update = (scaled / step_size[None, :, :, None]).reshape(proj_grads.shape)
    return (update, new_first, new_second)


def solution(mesh):
    in_specs = (
        P("dp", "tensor"),
        P("dp", "tensor"),
        P("dp", None, "tensor"),
        P("dp", "tensor"),
        P("dp", "tensor"),
        P("dp", "tensor"),
        P(),
        P(),
        P(("tensor", "dp"), None, None),
        P(),
    )
    out_specs = (P(("tensor", "dp"), None, None), P(("tensor", "dp"), None, None), P())
    return jax.shard_map(
        per_device, mesh=mesh, in_specs=in_specs, out_specs=out_specs, check_vma=False
    )
```

profile of v0, /device:TPU:0, one launch (start us, length us, event | category | flops | bytes accessed | tf_op | source)
XLA Modules:
  0.0 350.4 jit_solution(9090283319070825680)
XLA Ops:
  7.2 0.0 all-gather.2.cloned.1.call-start
  7.3 1.9 copy.44
  9.1 1.7 slice_bitcast_fusion.2
  10.8 1.7 slice_bitcast_fusion.6
  12.5 0.7 compare_bitcast_fusion
  13.3 2.6 reshape.151
  15.8 4.0 %reshape.152 = bf16[16,128,2,2,128]{4,3,2,1,0:T(2,128)(2,1)} reshape(bf16[2048,512]{1,0:T(8,128)(2,1)} %param.13) | data formatting | bytes 4194304 | tf_op jit(solution)/shard_map/reshape;reshape | solution.py:67
  19.8 0.1 broadcast_and_fusion.1
  19.9 0.1 broadcast_and_fusion
  20.1 0.1 and.20
  20.2 6.1 %fusion.107 = (bf16[16,128,1,2,128]{4,3,2,1,0:T(2,128)(2,1)S(1)}, bf16[16,128,1,2,128]{4,3,2,1,0:T(2,128)(2,1)}, bf16[16,128,1,2,128]{4,3,2,1,0:T(2,128)(2,1)S(1)}, bf16[16,128,1,2,128]{4,3,2,1,0:T(2,128)(2,1)S(1)}) fusion(bf16[16,128,2,2,128]{4,3,2,1,0:T(2,128)(2,1)} %reshape.152, bf16[16,128,2,2,128]{4,3,2,1,0:T(2,128)(2,1)S(1)} %reshape.151), kind=kLoop, calls=%fused_computation.126 | loop fusion | bytes 8388608 | tf_op jit(solution)/shard_map/slice | solution.py:76
  26.4 0.9 copy-done.4
  27.3 0.7 fusion.39
  28.1 2.5 fusion.31
  30.6 0.3 copy-done.3
  30.8 0.2 copy-done.18
  31.1 6.2 %bitcast_multiply_fusion.1 = f32[16,256,128]{2,1,0:T(8,128)} fusion(f32[16,256,128,2]{2,1,3,0:T(8,128)} %copy-done.3, f32[16,2,128]{2,1,0:T(2,128)S(1)} %get-tuple-element.37, f32[16,2,128]{2,1,0:T(2,128)S(1)} %get-tuple-element.35, pred[16,128,256]{1,2,0:T(8,128)(4,1)} %copy-done.14, bf16[15,128,128]{2,1,0:T(8,128)(2,1)S(1)} %copy-done.18, ...), kind=kOutput, calls=%fused_computation.26 | convolution fusion | flops 546832384 | bytes 9961472 | tf_op jit(solution)/shard_map/sgqk,sqgd->skd/dot_general | solution.py:44
  37.3 1.4 slice.129
  38.6 1.4 fusion.59
  40.1 0.2 copy.51
  40.3 0.7 fusion.47
  41.1 0.5 copy-done.11
  41.5 0.1 copy-done.15
  41.6 2.5 fusion.34
  44.2 6.1 %bitcast_multiply_fusion = f32[16,256,128]{2,1,0:T(8,128)} fusion(f32[16,256,128,2]{2,1,3,0:T(8,128)} %copy-done.2, f32[16,2,128]{2,1,0:T(2,128)S(1)} %get-tuple-element.36, f32[16,2,128]{2,1,0:T(2,128)S(1)} %get-tuple-element.34, pred[16,128,256]{1,2,0:T(8,128)(4,1)S(1)} %copy-done.16, bf16[15,128,128]{2,1,0:T(8,128)(2,1)} %get-tuple-element.21, ...), kind=kOutput, calls=%fused_computation.25 | convolution fusion | flops 546832384 | bytes 9961472 | tf_op jit(solution)/shard_map/sgqk,sqgd->skd/dot_general | solution.py:44
  50.2 1.3 slice.141
  51.5 1.4 fusion.54
  52.9 0.2 copy.57
  53.2 1.3 slice.131
  54.5 1.4 fusion.58
  55.9 0.2 copy.52
  56.1 1.3 slice.143
  57.4 1.4 fusion.53
  58.8 0.2 copy.58
  59.0 1.5 maximum_maximum_fusion
  60.6 0.0 reduce-scatter.2.cloned.1.call-start
  60.7 152.4 %all-gather.2.cloned.1.call-done = bf16[2048,2,1024]{0,2,1:T(8,128)(2,1)} async-done(((bf16[2048,2,256]{0,2,1:T(8,128)(2,1)}), bf16[2048,2,1024]{0,2,1:T(8,128)(2,1)}) %all-gather.2.cloned.1.call-update) | async-done | bytes 8388624 | tf_op jit(solution)/shard_map/all_gather | solution.py:114
  213.1 14.4 %fusion.10 = f32[1024,2,1024]{0,2,1:T(8,128)} fusion(bf16[2048,2,1024]{0,2,1:T(8,128)(2,1)} %all-gather.2.cloned.1.call-done, bf16[2048,1024]{1,0:T(8,128)(2,1)} %param.10), kind=kOutput, calls=%fused_computation.14 | convolution fusion | flops 8589934592 | bytes 20971520 | tf_op jit(solution)/shard_map/tr,tkc->rkc/dot_general | solution.py:111
  227.5 69.6 %reduce-scatter.2.cloned.1.call-done = f32[128,2,1024]{0,2,1:T(8,128)} async-done(((f32[1024,2,1024]{0,2,1:T(8,128)}), f32[128,2,1024]{0,2,1:T(8,128)}) %reduce-scatter.2.cloned.1.call-update) | async-done | bytes 1048592 | tf_op jit(solution)/shard_map/reduce_scatter | solution.py:117
  297.1 1.6 multiply_reduce_fusion
  298.7 0.1 bitcast_reduce_fusion
  298.8 0.5 copy.43
  299.3 39.3 %psum.7 = f32[2,8]{1,0:T(2,128)S(1)} all-reduce(f32[2,8]{1,0:T(2,128)S(1)} %bitcast_reduce_fusion), channel_id=1, replica_groups=mesh['dp'=8,'tensor'=4] {'dp','tensor'}, use_global_device_ids=true, to_apply=%region_3.4 | all-reduce | flops 16 | bytes 128 | tf_op jit(solution)/shard_map/psum | solution.py:124
  338.6 0.6 sqrt_add_fusion
  339.2 0.1 broadcast_bitcast_fusion
  339.3 1.6 multiply_divide_fusion
  340.9 1.3 copy.59
  342.2 1.3 copy.60
  (51 shorter events, 0.2 us)
Async XLA Ops:
  7.2 6.1 %copy-start = (s32[8,16]{1,0:T(8,128)S(1)}, s32[8,16]{1,0:T(8,128)}, u32[]{:S(2)}) copy-start(s32[8,16]{1,0:T(8,128)} %param.16) | copy-start | bytes 1540
  7.2 205.9 %all-gather.2.cloned.1.call-start = ((), (), s32[]{:S(2)}) async-start(), calls=%async_computation.1 | async-start | bytes 10485760 | tf_op jit(solution)/shard_map/all_gather | solution.py:114
  13.2 6.6 %copy-start.19 = (bf16[2048,4]{0,1:T(4,128)(2,1)S(1)}, bf16[2048,4]{0,1:T(4,128)(2,1)}, u32[]{:S(2)}) copy-start(bf16[2048,4]{0,1:T(4,128)(2,1)} %param.14) | copy-start | bytes 49156
  13.2 6.6 %copy-start.20 = (bf16[2048,4]{0,1:T(4,128)(2,1)S(1)}, bf16[2048,4]{0,1:T(4,128)(2,1)}, u32[]{:S(2)}) copy-start(bf16[2048,4]{0,1:T(4,128)(2,1)} %param.15) | copy-start | bytes 49156
  20.2 7.9 %copy-start.14 = (pred[16,128,256]{1,2,0:T(8,128)(4,1)}, pred[16,128,256]{1,2,0:T(8,128)(4,1)S(1)}, u32[]{:S(2)}) copy-start(pred[16,128,256]{1,2,0:T(8,128)(4,1)S(1)} %pad_add_fusion) | copy-start | bytes 1572868
  20.2 7.1 %copy-start.7 = (bf16[16,128,128]{2,1,0:T(8,128)(2,1)S(1)}, bf16[16,128,128]{2,1,0:T(8,128)(2,1)}, u32[]{:S(2)}) copy-start(bf16[16,128,128]{2,1,0:T(8,128)(2,1)} %get-tuple-element.19) | copy-start | bytes 1572868
  20.2 7.1 %copy-start.9 = (bf16[15,128,128]{2,1,0:T(8,128)(2,1)S(1)}, bf16[15,128,128]{2,1,0:T(8,128)(2,1)}, u32[]{:S(2)}) copy-start(bf16[15,128,128]{2,1,0:T(8,128)(2,1)} %get-tuple-element.23) | copy-start | bytes 1474564
  26.4 1.0 copy-start.4
  26.4 4.2 %copy-start.13 = (bf16[16,128,1,2,128]{4,3,2,1,0:T(2,128)(2,1)}, bf16[16,128,1,2,128]{4,3,2,1,0:T(2,128)(2,1)S(1)}, u32[]{:S(2)}) copy-start(bf16[16,128,1,2,128]{4,3,2,1,0:T(2,128)(2,1)S(1)} %get-tuple-element.24) | copy-start | bytes 3145732
  28.0 2.8 copy-start.3
  28.1 2.8 copy-start.5
  28.1 2.8 copy-start.17
  28.1 3.0 copy-start.18
  37.3 3.0 copy-start.6
  37.3 3.1 copy-start.8
  40.3 1.2 copy-start.11
  40.3 1.3 copy-start.15
  41.0 3.1 copy-start.2
  41.6 2.5 copy-start.12
  41.6 2.5 copy-start.16
  60.6 236.5 %reduce-scatter.2.cloned.1.call-start = ((), (), s32[]{:S(2)}) async-start(), calls=%async_computation.2 | async-start | bytes 9437184 | tf_op jit(solution)/shard_map/reduce_scatter | solution.py:117
  227.5 71.3 %copy-start.10 = (f32[128,2,1024]{2,1,0:T(2,128)S(1)}, f32[128,2,1024]{2,1,0:T(2,128)}, u32[]{:S(2)}) copy-start(f32[128,2,1024]{2,1,0:T(2,128)} %param.18) | copy-start | bytes 3145732
  227.5 111.1 %copy-start.21 = (f32[2,8]{1,0:T(2,128)S(1)}, f32[2,8]{1,0:T(2,128)}, u32[]{:S(2)}) copy-start(f32[2,8]{1,0:T(2,128)} %param.19) | copy-start | bytes 196
  339.3 4.2 %copy-start.1 = (s32[8,16]{1,0:T(8,128)S(1)}, s32[8,16]{1,0:T(8,128)}, u32[]{:S(2)}) copy-start(s32[8,16]{1,0:T(8,128)} %param.16) | copy-start | bytes 1540
Sparse Core Ops, SparseCore 0:
  60.7 152.3 all-gather.1
  227.6 69.4 reduce-scatter.1
where the time goes:
time: 351 us; the launch traced here: 350 us
  waiting for transfers between devices  222 us (63%)
  blocking collectives  39.3 us (11%)
  matrix products  33 us (9%)
  local copies, waits for them, and re-layouts  29.4 us (8%)
  between operations  14.4 us (4%)
  other arithmetic  12.1 us (3%)
    all_gather x1, waiting for transfers between devices, per_device(): lax.all_gather(kv_grads, 'tensor', axis=2, tiled=True)  152 us
    reduce_scatter x1, waiting for transfers between devices, per_device(): summed = lax.psum_scatter(terms, 'dp', scatter_dimension=0, tiled=True)  69.6 us
    psum x1, blocking collectives, per_device(): squares = lax.psum(partial_squares, ('dp', 'tensor'))  39.3 us
    dot_general x1, matrix products, per_device(): jnp.einsum('tr,tkc->rkc', layer_input, lax.all_gather(kv_grads, 'tensor',...  14.4 us
    dot_general x2, matrix products, band_grads(): jnp.einsum('sgqk,sqgd->skd', dscores.astype(jnp.bfloat16), q_tiles, prefe...  12.3 us
    unnamed x52, local copies, waits for them, and re-layouts  7.17 us
  transfers between devices with their start and end apart: 2, of which 2 were waited for; matrix products, arithmetic and copies ran while one was open for 0% of the time, Pallas kernels for 0%

commit v1 on v0

--- a/solution.py
+++ b/solution.py
@@ -9,6 +9,18 @@
 ADAM_ONE = 0.9
 ADAM_TWO = 0.95
 ADAM_EPS = 1e-08
+
+
+def doubled_up(value, axis, dim):
+    ways, here, step = (lax.axis_size(axis), lax.axis_index(axis), value.shape[dim])
+    line, have = (value, 1)
+    while have < ways:
+        line = jnp.concatenate(
+            [line, lax.ppermute(line, axis, [(d, (d - have) % ways) for d in range(ways)])],
+            axis=dim,
+        )
+        have = 2 * have
+    return jnp.roll(line, here * step, axis=dim)
 
 
 def band_grads(q_tiles, k_tiles, v_tiles, do_tiles, lse_tiles, delta_tiles, fill_tiles, cont_tiles):
@@ -111,7 +123,7 @@
     terms = jnp.einsum(
         "tr,tkc->rkc",
         layer_input,
-        lax.all_gather(kv_grads, "tensor", axis=2, tiled=True),
+        doubled_up(kv_grads, "tensor", 2),
         preferred_element_type=jnp.float32,
     )
     summed = lax.psum_scatter(terms, "dp", scatter_dimension=0, tiled=True)

time: 351 us -> 441 us (1.26)
  waiting for transfers between devices: 222 us -> 295 us
  local copies, waits for them, and re-layouts: 29.4 us -> 36.7 us
  starting transfers between devices: 0.08 us -> 6.63 us
  other arithmetic: 12.1 us -> 17.1 us
    ppermute x0 -> x2, waiting for transfers between devices: none -> 224 us  [doubled_up(): lax.ppermute(line, axis, [(d, (d - have) % ways) for d in range(ways)])]
    all_gather x1 -> x0, waiting for transfers between devices: 152 us -> none  [per_device(): lax.all_gather(kv_grads, 'tensor', axis=2, tiled=True)]
    ppermute x0 -> x2, starting transfers between devices: none -> 6.59 us  [doubled_up(): lax.ppermute(line, axis, [(d, (d - have) % ways) for d in range(ways)])]
    unnamed x52 -> x59, local copies, waits for them, and re-layouts: 7.17 us -> 10.6 us
  transfers between devices with their start and end apart: 2 -> 3, of which waited for: 2 -> 3; matrix products, arithmetic and copies ran while one was open for 0% -> 1% of each run, Pallas kernels for 0% -> 0%
where the time goes in v1:
time: 441 us; the launch traced here: 440 us
  waiting for transfers between devices  295 us (67%)
  blocking collectives  39.3 us (9%)
  local copies, waits for them, and re-layouts  36.7 us (8%)
  matrix products  30.7 us (7%)
  other arithmetic  17.1 us (4%)
  between operations  14.5 us (3%)
  starting transfers between devices  6.63 us (2%)
    ppermute x2, waiting for transfers between devices, doubled_up(): lax.ppermute(line, axis, [(d, (d - have) % ways) for d in range(ways)])  224 us
    reduce_scatter x1, waiting for transfers between devices, per_device(): summed = lax.psum_scatter(terms, 'dp', scatter_dimension=0, tiled=True)  71.5 us
    psum x1, blocking collectives, per_device(): squares = lax.psum(partial_squares, ('dp', 'tensor'))  39.3 us
    dot_general x2, matrix products, band_grads(): jnp.einsum('sgqk,sqgd->skd', dscores.astype(jnp.bfloat16), q_tiles, prefe...  12.1 us
    dot_general x1, matrix products, per_device(): jnp.einsum('tr,tkc->rkc', layer_input, doubled_up(kv_grads, 'tensor', 2),...  11 us
    unnamed x59, local copies, waits for them, and re-layouts  10.6 us
  transfers between devices with their start and end apart: 3, of which 3 were waited for; matrix products, arithmetic and copies ran while one was open for 1% of the time, Pallas kernels for 0%

profile of v1, /device:TPU:0, one launch (start us, length us, event | category | flops | bytes accessed | tf_op | source)
XLA Modules:
  0.0 440.0 jit_solution(1646832624500487148)
XLA Ops:
  7.3 1.9 copy.44
  9.1 1.7 slice_bitcast_fusion
  10.9 1.6 slice_bitcast_fusion.4
  12.5 0.7 compare_bitcast_fusion
  13.2 2.6 reshape.151
  15.8 4.0 reshape.152
  19.9 0.1 broadcast_and_fusion
  20.2 7.1 %fusion.116 = (bf16[16,128,1,2,128]{4,3,2,1,0:T(2,128)(2,1)S(1)}, bf16[16,128,1,2,128]{4,3,2,1,0:T(2,128)(2,1)}, bf16[16,128,1,2,128]{4,3,2,1,0:T(2,128)(2,1)}, bf16[16,128,1,2,128]{4,3,2,1,0:T(2,128)(2,1)S(1)}) fusion(bf16[16,128,2,2,128]{4,3,2,1,0:T(2,128)(2,1)} %reshape.152, bf16[16,128,2,2,128]{4,3,2,1,0:T(2,128)(2,1)S(1)} %reshape.151), kind=kLoop, calls=%fused_computation.141 | loop fusion | bytes 8388608 | tf_op jit(solution)/shard_map/slice | solution.py:88
  27.3 0.7 fusion.50
  28.1 2.6 fusion.37
  30.7 6.1 %bitcast_multiply_fusion = f32[16,256,128]{2,1,0:T(8,128)} fusion(f32[16,256,128,2]{2,1,3,0:T(8,128)} %copy-done.7, f32[16,2,128]{2,1,0:T(2,128)S(1)} %get-tuple-element.36, f32[16,2,128]{2,1,0:T(2,128)S(1)} %get-tuple-element.34, pred[16,128,256]{1,2,0:T(8,128)(4,1)} %copy-done.16, bf16[15,128,128]{2,1,0:T(8,128)(2,1)S(1)} %copy-done.19, ...), kind=kOutput, calls=%fused_computation.27 | convolution fusion | flops 546832384 | bytes 9961472 | tf_op jit(solution)/shard_map/sgqk,sqgd->skd/dot_general | solution.py:56
  36.8 1.4 slice.141
  38.2 1.4 fusion.57
  39.6 0.2 copy.57
  39.9 1.8 fusion.42
  41.7 2.4 fusion.34
  44.3 6.0 %bitcast_multiply_fusion.1 = f32[16,256,128]{2,1,0:T(8,128)} fusion(f32[16,256,128,2]{2,1,3,0:T(8,128)} %copy-done.6, f32[16,2,128]{2,1,0:T(2,128)S(1)} %get-tuple-element.37, f32[16,2,128]{2,1,0:T(2,128)S(1)} %get-tuple-element.35, pred[16,128,256]{1,2,0:T(8,128)(4,1)S(1)} %copy-done.17, bf16[15,128,128]{2,1,0:T(8,128)(2,1)} %get-tuple-element.22, ...), kind=kOutput, calls=%fused_computation.28 | convolution fusion | flops 546832384 | bytes 9961472 | tf_op jit(solution)/shard_map/sgqk,sqgd->skd/dot_general | solution.py:56
  50.3 1.3 slice.129
  51.6 1.3 fusion.62
  52.9 0.2 copy.51
  53.1 1.3 slice.143
  54.4 1.3 fusion.56
  55.8 0.2 copy.58
  56.0 1.5 slice.131
  57.4 1.3 fusion.61
  58.8 0.2 copy.52
  59.0 0.8 copy-done.4
  59.8 0.2 maximum_maximum_fusion
  60.0 5.1 %collective-permute-start = (bf16[2048,2,256]{0,2,1:T(8,128)(2,1)S(1)}, bf16[2048,2,256]{0,2,1:T(8,128)(2,1)S(1)}, u32[]{:S(2)}, u32[]{:S(2)}) collective-permute-start(bf16[2048,2,256]{0,2,1:T(8,128)(2,1)S(1)} %maximum_maximum_fusion), channel_id=1, source_target_pairs={{0,3},{1,0},{2,1},{3,2},{4,7},{5,4},{6,5},{7,6},{8,11},{9,8},{10,9... | collective-permute-start | bytes 6291464 | tf_op jit(solution)/shard_map/ppermute | solution.py:19
  65.1 44.9 %collective-permute-done = bf16[2048,2,256]{0,2,1:T(8,128)(2,1)S(1)} collective-permute-done((bf16[2048,2,256]{0,2,1:T(8,128)(2,1)S(1)}, bf16[2048,2,256]{0,2,1:T(8,128)(2,1)S(1)}, u32[]{:S(2)}, u32[]{:S(2)}) %collective-permute-start) | collective-permute-done | bytes 2097184 | tf_op jit(solution)/shard_map/ppermute | solution.py:19
  110.0 3.3 pad_maximum_fusion
  113.3 1.5 collective-permute-start.1
  114.8 1.1 fusion.79
  115.9 1.1 fusion.81
  117.1 0.1 constant_dynamic-update-slice_fusion.3
  117.3 178.6 %collective-permute-done.1 = bf16[2048,2,512]{0,2,1:T(8,128)(2,1)} collective-permute-done((bf16[2048,2,512]{0,2,1:T(8,128)(2,1)}, bf16[2048,2,512]{0,2,1:T(8,128)(2,1)}, u32[]{:S(2)}, u32[]{:S(2)}) %collective-permute-start.1) | collective-permute-done | bytes 4194336 | tf_op jit(solution)/shard_map/ppermute | solution.py:19
  295.9 2.7 constant_dynamic-update-slice_fusion.2
  299.0 2.9 constant_dynamic-update-slice_fusion
  301.8 0.6 copy-done.23
  302.4 11.0 %fusion.11 = f32[1024,2,1024]{0,2,1:T(8,128)} fusion(bf16[2048,1024]{1,0:T(8,128)(2,1)S(1)} %copy-done.23, bf16[2048,2,2048]{0,2,1:T(8,128)(2,1)S(1)} %constant_dynamic-update-slice_fusion, s32[]{:T(128)S(6)} %select_n.29), kind=kOutput, calls=%fused_computation.16 | convolution fusion | flops 8589934592 | bytes 20971524 | tf_op jit(solution)/shard_map/tr,tkc->rkc/dot_general | solution.py:123
  313.4 71.5 %reduce-scatter.2.cloned.1.call-done = f32[128,2,1024]{0,2,1:T(8,128)} async-done(((f32[1024,2,1024]{0,2,1:T(8,128)}), f32[128,2,1024]{0,2,1:T(8,128)}) %reduce-scatter.2.cloned.1.call-update) | async-done | bytes 1048592 | tf_op jit(solution)/shard_map/reduce_scatter | solution.py:129
  384.9 1.6 multiply_reduce_fusion
  386.6 0.5 copy.43
  387.1 39.3 %psum.7 = f32[2,8]{1,0:T(2,128)S(1)} all-reduce(f32[2,8]{1,0:T(2,128)S(1)} %bitcast_reduce_fusion), channel_id=1, replica_groups=mesh['dp'=8,'tensor'=4] {'dp','tensor'}, use_global_device_ids=true, to_apply=%region_3.4 | all-reduce | flops 16 | bytes 128 | tf_op jit(solution)/shard_map/psum | solution.py:136
  426.4 0.6 sqrt_add_fusion
  427.0 2.6 multiply_divide_fusion
  429.6 2.3 copy.59
  431.8 1.3 copy.60
  (65 shorter events, 1.0 us)
Async XLA Ops:
  7.2 6.0 %copy-start = (s32[8,16]{1,0:T(8,128)S(1)}, s32[8,16]{1,0:T(8,128)}, u32[]{:S(2)}) copy-start(s32[8,16]{1,0:T(8,128)} %param.16) | copy-start | bytes 1540
  7.2 377.7 %reduce-scatter.2.cloned.1.call-start = ((), (), s32[]{:S(2)}) async-start(), calls=%async_computation.1 | async-start | bytes 9437184 | tf_op jit(solution)/shard_map/reduce_scatter | solution.py:129
  13.2 6.6 %copy-start.20 = (bf16[2048,4]{0,1:T(4,128)(2,1)S(1)}, bf16[2048,4]{0,1:T(4,128)(2,1)}, u32[]{:S(2)}) copy-start(bf16[2048,4]{0,1:T(4,128)(2,1)} %param.14) | copy-start | bytes 49156
  13.2 6.6 %copy-start.21 = (bf16[2048,4]{0,1:T(4,128)(2,1)S(1)}, bf16[2048,4]{0,1:T(4,128)(2,1)}, u32[]{:S(2)}) copy-start(bf16[2048,4]{0,1:T(4,128)(2,1)} %param.15) | copy-start | bytes 49156
  20.2 7.9 %copy-start.16 = (pred[16,128,256]{1,2,0:T(8,128)(4,1)}, pred[16,128,256]{1,2,0:T(8,128)(4,1)S(1)}, u32[]{:S(2)}) copy-start(pred[16,128,256]{1,2,0:T(8,128)(4,1)S(1)} %pad_add_fusion) | copy-start | bytes 1572868
  20.2 7.1 %copy-start.10 = (bf16[16,128,128]{2,1,0:T(8,128)(2,1)S(1)}, bf16[16,128,128]{2,1,0:T(8,128)(2,1)}, u32[]{:S(2)}) copy-start(bf16[16,128,128]{2,1,0:T(8,128)(2,1)} %get-tuple-element.17) | copy-start | bytes 1572868
  20.2 7.1 %copy-start.11 = (bf16[15,128,128]{2,1,0:T(8,128)(2,1)S(1)}, bf16[15,128,128]{2,1,0:T(8,128)(2,1)}, u32[]{:S(2)}) copy-start(bf16[15,128,128]{2,1,0:T(8,128)(2,1)} %get-tuple-element.21) | copy-start | bytes 1474564
  27.3 3.4 copy-start.15
  28.1 2.7 copy-start.7
  28.1 2.6 copy-start.18
  28.1 2.6 copy-start.19
  36.8 3.0 copy-start.8
  36.8 3.0 copy-start.9
  39.6 2.1 copy-start.17
  39.8 1.9 copy-start.13
  41.7 2.6 copy-start.6
  41.7 2.6 copy-start.14
  56.0 3.0 copy-start.2
  59.0 0.8 copy-start.4
  60.0 50.0 %collective-permute-start = (bf16[2048,2,256]{0,2,1:T(8,128)(2,1)S(1)}, bf16[2048,2,256]{0,2,1:T(8,128)(2,1)S(1)}, u32[]{:S(2)}, u32[]{:S(2)}) collective-permute-start(bf16[2048,2,256]{0,2,1:T(8,128)(2,1)S(1)} %maximum_maximum_fusion), channel_id=1, source_target_pairs={{0,3},{1,0},{2,1},{3,2},{4,7},{5,4},{6,5},{7,6},{8,11},{9,8},{10,9... | collective-permute-start | bytes 6291464 | tf_op jit(solution)/shard_map/ppermute | solution.py:19
  113.3 182.6 %collective-permute-start.1 = (bf16[2048,2,512]{0,2,1:T(8,128)(2,1)}, bf16[2048,2,512]{0,2,1:T(8,128)(2,1)}, u32[]{:S(2)}, u32[]{:S(2)}) collective-permute-start(bf16[2048,2,512]{0,2,1:T(8,128)(2,1)} %pad_maximum_fusion), channel_id=1, source_target_pairs={{0,2},{1,3},{2,0},{3,1},{4,6},{5,7},{6,4},{7,5},{8,10},{9,11},{10,... | collective-permute-start | bytes 12582920 | tf_op jit(solution)/shard_map/ppermute | solution.py:19
  117.2 181.4 %copy-start.5 = (bf16[2048,1,128]{0,2,1:T(8,128)(2,1)S(1)}, bf16[2048,1,128]{0,2,1:T(8,128)(2,1)}, u32[]{:S(2)}) copy-start(bf16[2048,1,128]{0,2,1:T(8,128)(2,1)} %copy-done.4) | copy-start | bytes 1572868
  117.2 181.4 %copy-start.3 = (bf16[2048,1,128]{0,2,1:T(8,128)(2,1)S(1)}, bf16[2048,1,128]{0,2,1:T(8,128)(2,1)}, u32[]{:S(2)}) copy-start(bf16[2048,1,128]{0,2,1:T(8,128)(2,1)} %copy-done.2) | copy-start | bytes 1572868
  298.9 3.5 copy-start.23
  313.4 73.1 %copy-start.12 = (f32[128,2,1024]{2,1,0:T(2,128)S(1)}, f32[128,2,1024]{2,1,0:T(2,128)}, u32[]{:S(2)}) copy-start(f32[128,2,1024]{2,1,0:T(2,128)} %param.18) | copy-start | bytes 3145732
  313.4 113.0 %copy-start.22 = (f32[2,8]{1,0:T(2,128)S(1)}, f32[2,8]{1,0:T(2,128)}, u32[]{:S(2)}) copy-start(f32[2,8]{1,0:T(2,128)} %param.19) | copy-start | bytes 196
  427.0 6.1 %copy-start.1 = (s32[8,16]{1,0:T(8,128)S(1)}, s32[8,16]{1,0:T(8,128)}, u32[]{:S(2)}) copy-start(s32[8,16]{1,0:T(8,128)} %param.16) | copy-start | bytes 1540
Sparse Core Ops, SparseCore 0:
  313.6 71.2 reduce-scatter.1
